TPU v7x, 32 devices: a whole 2x2x4 slice. The times are simulated.
32 devices in a mesh: wav: 8 (over y, x, core), lev: 4 (over z).
Axes of the slice: x: 2, y: 2, z: 4, core: 2. Of those that a mesh axis runs over, the one named last changes fastest.
Arguments:
- spectral: bfloat16 [200, 401, 512], P('wav', None, 'lev'), may hold values from -0.1796875 to 0.1796875
- legendre: bfloat16 [200, 401, 64], P('wav', None, 'lev'), may hold values from -0.4375 to 0.4375
- wave_pair: int32 [200], replicated, may hold values from -1 to 199, as said below
- lat_slot: int32 [64], replicated, may hold values from 0 to 799, as said below
Outputs:
- gridded: bfloat16 [64, 256, 1616], P('wav', 'lev')
Inputs may be any that keep to these rules, and one draw needn't show every extreme that they name: `wave_pair`: each pair number 0 to 199 appears exactly once; all other entries are -1. `lat_slot`: the entries are distinct latitudes.
All inputs are finite; a program needn't handle non-finite values.
Results may differ from a plain program's by a relative error of at most 0.0055.
Values may be sent and summed in bfloat16 or wider, within the bound.
A program may use at most 64 MiB of HBM per device.

v0:
```python
import math
import jax
import jax.numpy as jnp
from jax import lax
from jax.sharding import PartitionSpec as P

NLAT = 800


def fold_masks(pair_ids, fold_count, wave_count):
    fold_rows = jnp.arange(fold_count, dtype=jnp.int32)
    filled = pair_ids >= 0
    border = wave_count - pair_ids
    lower = filled[:, None] & (fold_rows[None, :] < border[:, None])
    upper = filled[:, None] & (fold_rows[None, :] >= border[:, None])
    return jnp.stack([lower, upper], axis=1)


def trig_parts(wave_numbers, steps, counts_b):
    residue = wave_numbers[None, None] * steps[None, :, None, None] % counts_b
    angles = residue.astype(jnp.float32) * (2.0 * math.pi) / counts_b.astype(jnp.float32)
    return (jnp.cos(angles), jnp.sin(angles))


def synthesis_table(pair_ids, row_lats, lat_count, lon_width, wave_count):
    filled = pair_ids >= 0
    wave_numbers = jnp.stack([pair_ids, wave_count - 1 - pair_ids], axis=1)
    lon_count = 20 + 4 * jnp.minimum(row_lats, lat_count - 1 - row_lats)
    highest = jnp.minimum(wave_count - 1, (lon_count - 1) // 2)
    counts_b = lon_count[:, None, None, None]
    coarse_count = (lon_width + 63) // 64
    coarse_steps = jnp.arange(coarse_count, dtype=jnp.int32) * 64
    fine_steps = jnp.arange(64, dtype=jnp.int32)
    cos_coarse, sin_coarse = trig_parts(wave_numbers, coarse_steps, counts_b)
    cos_fine, sin_fine = trig_parts(wave_numbers, fine_steps, counts_b)
    cos_all = (
        cos_coarse[:, :, None] * cos_fine[:, None] - sin_coarse[:, :, None] * sin_fine[:, None]
    )
    sin_all = (
        sin_coarse[:, :, None] * cos_fine[:, None] + cos_coarse[:, :, None] * sin_fine[:, None]
    )
    row_total = row_lats.shape[0]
    cos_all = cos_all.reshape(row_total, coarse_count * 64, wave_numbers.shape[0], 2)[:, :lon_width]
    sin_all = sin_all.reshape(row_total, coarse_count * 64, wave_numbers.shape[0], 2)[:, :lon_width]
    columns = jnp.arange(lon_width, dtype=jnp.int32)
    valid = (
        filled[None, None, :, None]
        & (wave_numbers[None, None] <= highest[:, None, None, None])
        & (columns[None, :, None, None] < counts_b)
    )
    factor = jnp.where(wave_numbers == 0, 1.0, 2.0).astype(jnp.float32)[None, None]
    real_part = jnp.where(valid, factor * cos_all, 0.0)
    imag_part = jnp.where(valid, -factor * sin_all, 0.0)
    return jnp.stack([real_part, imag_part], axis=-1).astype(jnp.bfloat16)


def legendre_sum(coefficients, weights, half_masks):
    paired = coefficients.reshape(
        coefficients.shape[0], coefficients.shape[1], coefficients.shape[2] // 2, 2
    )
    masked = jnp.where(
        half_masks[:, :, :, None, None], paired[:, None], jnp.zeros((), paired.dtype)
    )
    summed = jnp.einsum("shtlc,sta->ashcl", masked, weights, preferred_element_type=jnp.float32)
    return summed.astype(jnp.bfloat16)


def on_device(spectral, legendre, wave_pair, lat_slot):
    slot_count = spectral.shape[0]
    fold_count = spectral.shape[1]
    wave_count = fold_count - 1
    lat_count = NLAT
    lon_width = 2 * lat_count + 16
    wav_devices = lax.axis_size("wav")
    wav_index = lax.axis_index("wav")
    own_pairs = lax.dynamic_slice_in_dim(wave_pair, wav_index * slot_count, slot_count)
    half_masks = fold_masks(own_pairs, fold_count, wave_count)
    fourier = legendre_sum(
        spectral, lax.all_gather(legendre, "lev", axis=2, tiled=True), half_masks
    )
    row_count = lat_slot.shape[0] // wav_devices
    row_lats = lax.dynamic_slice_in_dim(lat_slot, wav_index * row_count, row_count)
    group_rows = max(1, row_count // 25)
    while row_count % group_rows:
        group_rows -= 1
    group_count = row_count // group_rows
    received = lax.all_to_all(fourier, "wav", split_axis=0, concat_axis=1, tiled=True)
    layer_items = received.shape[4]
    grouped = received.reshape((group_count, group_rows) + received.shape[1:])
    lat_groups = row_lats.reshape(group_count, group_rows)

    def one_group(args):
        values, group_lats = args
        basis = synthesis_table(wave_pair, group_lats, lat_count, lon_width, wave_count)
        result = jnp.einsum("rjghc,rghcl->rlj", basis, values, preferred_element_type=jnp.float32)
        return result.astype(jnp.bfloat16)

    gridded_groups = lax.map(one_group, (grouped, lat_groups))
    return gridded_groups.reshape(row_count, layer_items, lon_width)


def solution(mesh):
    return jax.shard_map(
        on_device,
        mesh=mesh,
        in_specs=(P("wav", None, "lev"), P("wav", None, "lev"), P(), P()),
        out_specs=P("wav", "lev", None),
        check_vma=False,
    )
```

profile of v0, /device:TPU:0, one launch (start us, length us, event | category | flops | bytes accessed | tf_op | source)
XLA Modules:
  0.0 257.9 jit_solution(4773059625746741273)
XLA Ops:
  7.3 5.4 %copy.16 = bf16[25,401,128]{1,2,0:T(8,128)(2,1)} copy(bf16[25,401,128]{2,1,0:T(8,128)(2,1)} %param.6) | data formatting | bytes 5132800 | tf_op args[0]
  12.7 6.7 %broadcast_in_dim.92 = bf16[25,401,64,2]{1,3,2,0:T(2,128)(2,1)S(1)} reshape(bf16[25,401,128]{1,2,0:T(8,128)(2,1)} %copy.16) | data formatting | bytes 5132800 | tf_op jit(solution)/shard_map/jit(_where)/broadcast_in_dim | solution.py:61
  22.3 27.4 %all-gather.2.cloned.1.call-done = bf16[25,401,64]{1,2,0:T(8,128)(2,1)} async-done(((bf16[25,401,16]{1,2,0:T(8,128)(2,1)}), bf16[25,401,64]{1,2,0:T(8,128)(2,1)}) %all-gather.2.cloned.1.call-update) | async-done | bytes 1283216 | tf_op jit(solution)/shard_map/all_gather | solution.py:79
  49.8 4.3 %fusion.52 = bf16[64,25,2,2,64]{0,4,3,2,1:T(8,128)(2,1)S(1)} fusion(bf16[25,401,64]{1,2,0:T(8,128)(2,1)} %all-gather.2.cloned.1.call-done, pred[25,2,401]{2,1,0:T(4,128)(4,1)S(1)} %pad_add_fusion.1, bf16[25,401,64,2]{1,2,3,0:T(8,128)(2,1)} %copy.17), kind=kOutput, calls=%fused_computation.59 | convolution fusion | flops 331475200 | bytes 4688850 | tf_op jit(solution)/shard_map/shtlc,sta->ashcl/dot_general | solution.py:64
  54.0 3.0 %copy.18 = bf16[64,25,2,2,64]{4,3,2,1,0:T(2,128)(2,1)S(1)} copy(bf16[64,25,2,2,64]{0,4,3,2,1:T(8,128)(2,1)S(1)} %fusion.52) | data formatting | bytes 1638400 | tf_op jit(solution)/shard_map/convert_element_type | solution.py:65
  58.9 3.7 %all-to-all-start = ((bf16[8,2,25600]{2,1,0:T(2,128)(2,1)}), bf16[8,2,25600]{2,1,0:T(2,128)(2,1)S(1)}, u32[]{:S(2)}, u32[]{:S(2)}) async-start(bf16[8,2,25600]{2,1,0:T(2,128)(2,1)} %reshape.584), calls=%async_computation | async-start | bytes 1638400 | tf_op jit(solution)/shard_map/all_to_all | solution.py:87
  62.7 12.7 %all-to-all-done = bf16[8,2,25600]{2,1,0:T(2,128)(2,1)S(1)} async-done(((bf16[8,2,25600]{2,1,0:T(2,128)(2,1)}), bf16[8,2,25600]{2,1,0:T(2,128)(2,1)S(1)}, u32[]{:S(2)}, u32[]{:S(2)}) %all-to-all-start) | async-done | bytes 819232 | tf_op jit(solution)/shard_map/all_to_all | solution.py:87
  79.6 171.5 %while.15 = (s32[]{:T(128)}, bf16[8,1,64,1616]{3,2,1,0:T(8,128)(2,1)}, bf16[8,1,200,2,2,64]{2,5,3,4,1,0:T(8,128)(2,1)}, s32[200]{0:T(256)S(1)}, s32[8,1]{0,1:T(1...) while((s32[]{:T(128)}, ...), condition=%wide.region_1.2_spmd, body=%wide.region_0.1_spmd.sunk | while | flops 175794288 | bytes 47638996 | solution.py:98
  87.0 3.5 %copy.30 = f32[1,1616,200,2]{1,2,3,0:T(8,128)} copy(f32[1,1616,200,2]{2,1,3,0:T(8,128)} %slice.24) | data formatting | bytes 5171200 | tf_op jit(solution)/shard_map/while
  92.4 3.7 %copy.31 = f32[1,1616,200,2]{1,2,3,0:T(8,128)} copy(f32[1,1616,200,2]{2,1,3,0:T(8,128)} %slice.25) | data formatting | bytes 5171200 | tf_op jit(solution)/shard_map/while
  96.2 2.5 fusion.68
  108.4 3.5 %copy.30 = f32[1,1616,200,2]{1,2,3,0:T(8,128)} copy(f32[1,1616,200,2]{2,1,3,0:T(8,128)} %slice.24) | data formatting | bytes 5171200 | tf_op jit(solution)/shard_map/while
  113.8 3.7 %copy.31 = f32[1,1616,200,2]{1,2,3,0:T(8,128)} copy(f32[1,1616,200,2]{2,1,3,0:T(8,128)} %slice.25) | data formatting | bytes 5171200 | tf_op jit(solution)/shard_map/while
  117.6 2.5 fusion.68
  129.8 3.5 %copy.30 = f32[1,1616,200,2]{1,2,3,0:T(8,128)} copy(f32[1,1616,200,2]{2,1,3,0:T(8,128)} %slice.24) | data formatting | bytes 5171200 | tf_op jit(solution)/shard_map/while
  135.3 3.7 %copy.31 = f32[1,1616,200,2]{1,2,3,0:T(8,128)} copy(f32[1,1616,200,2]{2,1,3,0:T(8,128)} %slice.25) | data formatting | bytes 5171200 | tf_op jit(solution)/shard_map/while
  139.1 2.5 fusion.68
  151.3 3.5 %copy.30 = f32[1,1616,200,2]{1,2,3,0:T(8,128)} copy(f32[1,1616,200,2]{2,1,3,0:T(8,128)} %slice.24) | data formatting | bytes 5171200 | tf_op jit(solution)/shard_map/while
  156.7 3.7 %copy.31 = f32[1,1616,200,2]{1,2,3,0:T(8,128)} copy(f32[1,1616,200,2]{2,1,3,0:T(8,128)} %slice.25) | data formatting | bytes 5171200 | tf_op jit(solution)/shard_map/while
  160.5 2.5 fusion.68
  172.7 3.5 %copy.30 = f32[1,1616,200,2]{1,2,3,0:T(8,128)} copy(f32[1,1616,200,2]{2,1,3,0:T(8,128)} %slice.24) | data formatting | bytes 5171200 | tf_op jit(solution)/shard_map/while
  178.1 3.7 %copy.31 = f32[1,1616,200,2]{1,2,3,0:T(8,128)} copy(f32[1,1616,200,2]{2,1,3,0:T(8,128)} %slice.25) | data formatting | bytes 5171200 | tf_op jit(solution)/shard_map/while
  181.9 2.5 fusion.68
  194.1 3.5 %copy.30 = f32[1,1616,200,2]{1,2,3,0:T(8,128)} copy(f32[1,1616,200,2]{2,1,3,0:T(8,128)} %slice.24) | data formatting | bytes 5171200 | tf_op jit(solution)/shard_map/while
  199.6 3.7 %copy.31 = f32[1,1616,200,2]{1,2,3,0:T(8,128)} copy(f32[1,1616,200,2]{2,1,3,0:T(8,128)} %slice.25) | data formatting | bytes 5171200 | tf_op jit(solution)/shard_map/while
  203.4 2.5 fusion.68
  215.6 3.5 %copy.30 = f32[1,1616,200,2]{1,2,3,0:T(8,128)} copy(f32[1,1616,200,2]{2,1,3,0:T(8,128)} %slice.24) | data formatting | bytes 5171200 | tf_op jit(solution)/shard_map/while
  221.0 3.7 %copy.31 = f32[1,1616,200,2]{1,2,3,0:T(8,128)} copy(f32[1,1616,200,2]{2,1,3,0:T(8,128)} %slice.25) | data formatting | bytes 5171200 | tf_op jit(solution)/shard_map/while
  224.8 2.5 fusion.68
  237.0 3.5 %copy.30 = f32[1,1616,200,2]{1,2,3,0:T(8,128)} copy(f32[1,1616,200,2]{2,1,3,0:T(8,128)} %slice.24) | data formatting | bytes 5171200 | tf_op jit(solution)/shard_map/while
  242.4 3.7 %copy.31 = f32[1,1616,200,2]{1,2,3,0:T(8,128)} copy(f32[1,1616,200,2]{2,1,3,0:T(8,128)} %slice.25) | data formatting | bytes 5171200 | tf_op jit(solution)/shard_map/while
  246.2 2.5 fusion.68
  (146 shorter events, 92.1 us)
Async XLA Ops:
  6.5 56.1 %copy-start = (s32[64]{0:T(128)S(1)}, s32[64]{0:T(128)}, u32[]{:S(2)}) copy-start(s32[64]{0:T(128)} %param.9) | copy-start | bytes 772
  6.5 43.2 %all-gather.2.cloned.1.call-start = ((), (), s32[]{:S(2)}) async-start(), calls=%async_computation.1 | async-start | bytes 2048000 | tf_op jit(solution)/shard_map/all_gather | solution.py:79
  19.4 2.4 copy-start.2
  58.9 16.6 %all-to-all-start = ((bf16[8,2,25600]{2,1,0:T(2,128)(2,1)}), bf16[8,2,25600]{2,1,0:T(2,128)(2,1)S(1)}, u32[]{:S(2)}, u32[]{:S(2)}) async-start(bf16[8,2,25600]{2,1,0:T(2,128)(2,1)} %reshape.584), calls=%async_computation | async-start | bytes 1638400 | tf_op jit(solution)/shard_map/all_to_all | solution.py:87
  92.4 3.8 %copy-start.1 = (f32[1,1616,200,2]{1,2,3,0:T(8,128)S(1)}, f32[1,1616,200,2]{1,2,3,0:T(8,128)}, u32[]{:S(2)}) copy-start(f32[1,1616,200,2]{1,2,3,0:T(8,128)} %copy.30) | copy-start | bytes 7756804 | tf_op jit(solution)/shard_map/while
  113.8 3.8 %copy-start.1 = (f32[1,1616,200,2]{1,2,3,0:T(8,128)S(1)}, f32[1,1616,200,2]{1,2,3,0:T(8,128)}, u32[]{:S(2)}) copy-start(f32[1,1616,200,2]{1,2,3,0:T(8,128)} %copy.30) | copy-start | bytes 7756804 | tf_op jit(solution)/shard_map/while
  135.3 3.8 %copy-start.1 = (f32[1,1616,200,2]{1,2,3,0:T(8,128)S(1)}, f32[1,1616,200,2]{1,2,3,0:T(8,128)}, u32[]{:S(2)}) copy-start(f32[1,1616,200,2]{1,2,3,0:T(8,128)} %copy.30) | copy-start | bytes 7756804 | tf_op jit(solution)/shard_map/while
  156.7 3.8 %copy-start.1 = (f32[1,1616,200,2]{1,2,3,0:T(8,128)S(1)}, f32[1,1616,200,2]{1,2,3,0:T(8,128)}, u32[]{:S(2)}) copy-start(f32[1,1616,200,2]{1,2,3,0:T(8,128)} %copy.30) | copy-start | bytes 7756804 | tf_op jit(solution)/shard_map/while
  178.1 3.8 %copy-start.1 = (f32[1,1616,200,2]{1,2,3,0:T(8,128)S(1)}, f32[1,1616,200,2]{1,2,3,0:T(8,128)}, u32[]{:S(2)}) copy-start(f32[1,1616,200,2]{1,2,3,0:T(8,128)} %copy.30) | copy-start | bytes 7756804 | tf_op jit(solution)/shard_map/while
  199.6 3.8 %copy-start.1 = (f32[1,1616,200,2]{1,2,3,0:T(8,128)S(1)}, f32[1,1616,200,2]{1,2,3,0:T(8,128)}, u32[]{:S(2)}) copy-start(f32[1,1616,200,2]{1,2,3,0:T(8,128)} %copy.30) | copy-start | bytes 7756804 | tf_op jit(solution)/shard_map/while
  221.0 3.8 %copy-start.1 = (f32[1,1616,200,2]{1,2,3,0:T(8,128)S(1)}, f32[1,1616,200,2]{1,2,3,0:T(8,128)}, u32[]{:S(2)}) copy-start(f32[1,1616,200,2]{1,2,3,0:T(8,128)} %copy.30) | copy-start | bytes 7756804 | tf_op jit(solution)/shard_map/while
  242.4 3.8 %copy-start.1 = (f32[1,1616,200,2]{1,2,3,0:T(8,128)S(1)}, f32[1,1616,200,2]{1,2,3,0:T(8,128)}, u32[]{:S(2)}) copy-start(f32[1,1616,200,2]{1,2,3,0:T(8,128)} %copy.30) | copy-start | bytes 7756804 | tf_op jit(solution)/shard_map/while
Sparse Core Ops, SparseCore 0:
  8.9 40.8 all-gather.1
where the time goes:
time: 259 us; the launch traced here: 258 us
  local copies, waits for them, and re-layouts  117 us (45%)
  other arithmetic  49.3 us (19%)
  waiting for transfers between devices  40.9 us (16%)
  matrix products  22.6 us (9%)
  between operations  13.5 us (5%)
  loops' own time  10.7 us (4%)
  starting transfers between devices  3.73 us (1%)
    while x32, local copies, waits for them, and re-layouts  58.4 us
    all_gather x1, waiting for transfers between devices, on_device(): lax.all_gather(legendre, 'lev', axis=2, tiled=True)  27.4 us
    cos x16, other arithmetic, trig_parts(): return (jnp.cos(angles), jnp.sin(angles))  22.2 us
    another operation x8, other arithmetic, synthesis_table(): return jnp.stack([real_part, imag_part], axis=-1).astype(jnp.bfloat16)  19.9 us
    dot_general x8, matrix products, one_group(): jnp.einsum('rjghc,rghcl->rlj', basis, values, preferred_element_type=jnp....  18.3 us
    slice x8, local copies, waits for them, and re-layouts, synthesis_table(): cos_all.reshape(row_total, coarse_count * 64, wave_numbers.shape[0], 2)  15.2 us
    slice x8, local copies, waits for them, and re-layouts, synthesis_table(): sin_all.reshape(row_total, coarse_count * 64, wave_numbers.shape[0], 2)  15.2 us
    all_to_all x1, waiting for transfers between devices, on_device(): lax.all_to_all(fourier, 'wav', split_axis=0, concat_axis=1, tiled=True)  12.7 us
  transfers between devices with their start and end apart: 2, of which 2 were waited for; matrix products, arithmetic and copies ran while one was open for 6% of the time, Pallas kernels for 0%

commit v1 on v0

--- a/solution.py
+++ b/solution.py
@@ -1,3 +1,4 @@
+import functools
 import math
 import jax
 import jax.numpy as jnp
@@ -5,6 +6,19 @@
 from jax.sharding import PartitionSpec as P
 
 NLAT = 800
+
+
+def recast_the_arrays(base_x, in_dim, ndim_at):
+    y2 = jnp.concatenate(
+        lax.all_to_all(
+            jnp.stack(jnp.split(base_x, lax.psum(1, "wav"), in_dim), axis=0), "wav", 0, 0
+        ),
+        axis=ndim_at,
+    )
+    return y2
+
+
+part_wires = functools.partial(recast_the_arrays, in_dim=0, ndim_at=1)
 
 
 def fold_masks(pair_ids, fold_count, wave_count):
@@ -84,7 +98,7 @@
     while row_count % group_rows:
         group_rows -= 1
     group_count = row_count // group_rows
-    received = lax.all_to_all(fourier, "wav", split_axis=0, concat_axis=1, tiled=True)
+    received = part_wires(fourier)
     layer_items = received.shape[4]
     grouped = received.reshape((group_count, group_rows) + received.shape[1:])
     lat_groups = row_lats.reshape(group_count, group_rows)

time: 259 us -> 257 us (level)
  local copies, waits for them, and re-layouts: 117 us -> 114 us
    convert_element_type x1 -> x0, local copies, waits for them, and re-layouts: 3 us -> none  [legendre_sum(): return summed.astype(jnp.bfloat16)]
    unnamed x7 -> x14, local copies, waits for them, and re-layouts: 8.24 us -> 8.73 us
where the time goes in v1:
time: 257 us; the launch traced here: 256 us
  local copies, waits for them, and re-layouts  114 us (44%)
  other arithmetic  49.3 us (19%)
  waiting for transfers between devices  40.9 us (16%)
  matrix products  24 us (9%)
  between operations  13.5 us (5%)
  loops' own time  10.7 us (4%)
  starting transfers between devices  3.73 us (1%)
    while x32, local copies, waits for them, and re-layouts  58.4 us
    all_gather x1, waiting for transfers between devices, on_device(): lax.all_gather(legendre, 'lev', axis=2, tiled=True)  27.4 us
    cos x16, other arithmetic, trig_parts(): return (jnp.cos(angles), jnp.sin(angles))  22.2 us
    another operation x8, other arithmetic, synthesis_table(): return jnp.stack([real_part, imag_part], axis=-1).astype(jnp.bfloat16)  19.9 us
    dot_general x8, matrix products, one_group(): jnp.einsum('rjghc,rghcl->rlj', basis, values, preferred_element_type=jnp....  18.3 us
    slice x8, local copies, waits for them, and re-layouts, synthesis_table(): cos_all.reshape(row_total, coarse_count * 64, wave_numbers.shape[0], 2)  15.2 us
    slice x8, local copies, waits for them, and re-layouts, synthesis_table(): sin_all.reshape(row_total, coarse_count * 64, wave_numbers.shape[0], 2)  15.2 us
    all_to_all x1, waiting for transfers between devices, recast_the_arrays(): lax.all_to_all(jnp.stack(jnp.split(base_x, lax.psum(1, 'wav'), in_dim), a...  12.7 us
  transfers between devices with their start and end apart: 2, of which 2 were waited for; matrix products, arithmetic and copies ran while one was open for 6% of the time, Pallas kernels for 0%

profile of v1, /device:TPU:0, one launch (start us, length us, event | category | flops | bytes accessed | tf_op | source)
XLA Modules:
  0.0 256.1 jit_solution(11682072765491706349)
XLA Ops:
  7.3 5.4 %copy.9 = bf16[25,401,128]{1,2,0:T(8,128)(2,1)} copy(bf16[25,401,128]{2,1,0:T(8,128)(2,1)} %param.6) | data formatting | bytes 5132800 | tf_op args[0]
  12.7 6.7 %broadcast_in_dim.92 = bf16[25,401,64,2]{1,3,2,0:T(2,128)(2,1)S(1)} reshape(bf16[25,401,128]{1,2,0:T(8,128)(2,1)} %copy.9) | data formatting | bytes 5132800 | tf_op jit(solution)/shard_map/jit(_where)/broadcast_in_dim | solution.py:75
  22.3 27.4 %all-gather.2.cloned.1.call-done = bf16[25,401,64]{1,2,0:T(8,128)(2,1)} async-done(((bf16[25,401,16]{1,2,0:T(8,128)(2,1)}), bf16[25,401,64]{1,2,0:T(8,128)(2,1)}) %all-gather.2.cloned.1.call-update) | async-done | bytes 1283216 | tf_op jit(solution)/shard_map/all_gather | solution.py:93
  49.8 5.7 %fusion.52 = bf16[64,25,2,2,64]{4,0,3,2,1:T(8,128)(2,1)S(1)} fusion(bf16[25,401,64]{1,2,0:T(8,128)(2,1)} %all-gather.2.cloned.1.call-done, pred[25,2,401]{2,1,0:T(4,128)(4,1)S(1)} %pad_add_fusion.1, bf16[25,401,64,2]{1,2,3,0:T(8,128)(2,1)} %copy.10), kind=kOutput, calls=%fused_computation.58 | convolution fusion | flops 331475200 | bytes 4688850 | tf_op jit(solution)/shard_map/shtlc,sta->ashcl/dot_general | solution.py:78
  57.8 3.7 %all-to-all-start = ((bf16[8,2,25600]{2,1,0:T(2,128)(2,1)}), bf16[8,2,25600]{2,1,0:T(2,128)(2,1)S(1)}, u32[]{:S(2)}, u32[]{:S(2)}) async-start(bf16[8,2,25600]{2,1,0:T(2,128)(2,1)} %reshape.583), calls=%async_computation | async-start | bytes 1638400 | tf_op jit(solution)/shard_map/all_to_all | solution.py:13
  61.7 12.7 %all-to-all-done = bf16[8,2,25600]{2,1,0:T(2,128)(2,1)S(1)} async-done(((bf16[8,2,25600]{2,1,0:T(2,128)(2,1)}), bf16[8,2,25600]{2,1,0:T(2,128)(2,1)S(1)}, u32[]{:S(2)}, u32[]{:S(2)}) %all-to-all-start) | async-done | bytes 819232 | tf_op jit(solution)/shard_map/all_to_all | solution.py:13
  75.4 2.4 copy.11
  77.8 171.5 %while.15 = (s32[]{:T(128)}, bf16[8,1,64,1616]{3,2,1,0:T(8,128)(2,1)}, bf16[8,1,200,2,2,64]{2,5,3,4,1,0:T(8,128)(2,1)}, s32[200]{0:T(256)S(1)}, s32[8,1]{0,1:T(1...) while((s32[]{:T(128)}, ...), condition=%wide.region_1.2_spmd, body=%wide.region_0.1_spmd.sunk | while | flops 175794288 | bytes 47638996 | solution.py:112
  85.2 3.5 %copy.18 = f32[1,1616,200,2]{1,2,3,0:T(8,128)} copy(f32[1,1616,200,2]{2,1,3,0:T(8,128)} %slice.24) | data formatting | bytes 5171200 | tf_op jit(solution)/shard_map/while
  90.6 3.7 %copy.19 = f32[1,1616,200,2]{1,2,3,0:T(8,128)} copy(f32[1,1616,200,2]{2,1,3,0:T(8,128)} %slice.25) | data formatting | bytes 5171200 | tf_op jit(solution)/shard_map/while
  94.5 2.5 fusion.76
  106.6 3.5 %copy.18 = f32[1,1616,200,2]{1,2,3,0:T(8,128)} copy(f32[1,1616,200,2]{2,1,3,0:T(8,128)} %slice.24) | data formatting | bytes 5171200 | tf_op jit(solution)/shard_map/while
  112.1 3.7 %copy.19 = f32[1,1616,200,2]{1,2,3,0:T(8,128)} copy(f32[1,1616,200,2]{2,1,3,0:T(8,128)} %slice.25) | data formatting | bytes 5171200 | tf_op jit(solution)/shard_map/while
  115.9 2.5 fusion.76
  128.1 3.5 %copy.18 = f32[1,1616,200,2]{1,2,3,0:T(8,128)} copy(f32[1,1616,200,2]{2,1,3,0:T(8,128)} %slice.24) | data formatting | bytes 5171200 | tf_op jit(solution)/shard_map/while
  133.5 3.7 %copy.19 = f32[1,1616,200,2]{1,2,3,0:T(8,128)} copy(f32[1,1616,200,2]{2,1,3,0:T(8,128)} %slice.25) | data formatting | bytes 5171200 | tf_op jit(solution)/shard_map/while
  137.3 2.5 fusion.76
  149.5 3.5 %copy.18 = f32[1,1616,200,2]{1,2,3,0:T(8,128)} copy(f32[1,1616,200,2]{2,1,3,0:T(8,128)} %slice.24) | data formatting | bytes 5171200 | tf_op jit(solution)/shard_map/while
  154.9 3.7 %copy.19 = f32[1,1616,200,2]{1,2,3,0:T(8,128)} copy(f32[1,1616,200,2]{2,1,3,0:T(8,128)} %slice.25) | data formatting | bytes 5171200 | tf_op jit(solution)/shard_map/while
  158.8 2.5 fusion.76
  170.9 3.5 %copy.18 = f32[1,1616,200,2]{1,2,3,0:T(8,128)} copy(f32[1,1616,200,2]{2,1,3,0:T(8,128)} %slice.24) | data formatting | bytes 5171200 | tf_op jit(solution)/shard_map/while
  176.4 3.7 %copy.19 = f32[1,1616,200,2]{1,2,3,0:T(8,128)} copy(f32[1,1616,200,2]{2,1,3,0:T(8,128)} %slice.25) | data formatting | bytes 5171200 | tf_op jit(solution)/shard_map/while
  180.2 2.5 fusion.76
  192.4 3.5 %copy.18 = f32[1,1616,200,2]{1,2,3,0:T(8,128)} copy(f32[1,1616,200,2]{2,1,3,0:T(8,128)} %slice.24) | data formatting | bytes 5171200 | tf_op jit(solution)/shard_map/while
  197.8 3.7 %copy.19 = f32[1,1616,200,2]{1,2,3,0:T(8,128)} copy(f32[1,1616,200,2]{2,1,3,0:T(8,128)} %slice.25) | data formatting | bytes 5171200 | tf_op jit(solution)/shard_map/while
  201.6 2.5 fusion.76
  213.8 3.5 %copy.18 = f32[1,1616,200,2]{1,2,3,0:T(8,128)} copy(f32[1,1616,200,2]{2,1,3,0:T(8,128)} %slice.24) | data formatting | bytes 5171200 | tf_op jit(solution)/shard_map/while
  219.2 3.7 %copy.19 = f32[1,1616,200,2]{1,2,3,0:T(8,128)} copy(f32[1,1616,200,2]{2,1,3,0:T(8,128)} %slice.25) | data formatting | bytes 5171200 | tf_op jit(solution)/shard_map/while
  223.1 2.5 fusion.76
  235.2 3.5 %copy.18 = f32[1,1616,200,2]{1,2,3,0:T(8,128)} copy(f32[1,1616,200,2]{2,1,3,0:T(8,128)} %slice.24) | data formatting | bytes 5171200 | tf_op jit(solution)/shard_map/while
  240.7 3.7 %copy.19 = f32[1,1616,200,2]{1,2,3,0:T(8,128)} copy(f32[1,1616,200,2]{2,1,3,0:T(8,128)} %slice.25) | data formatting | bytes 5171200 | tf_op jit(solution)/shard_map/while
  244.5 2.5 fusion.76
  (151 shorter events, 89.6 us)
Async XLA Ops:
  6.5 55.0 %copy-start = (s32[64]{0:T(128)S(1)}, s32[64]{0:T(128)}, u32[]{:S(2)}) copy-start(s32[64]{0:T(128)} %param.9) | copy-start | bytes 772
  6.5 43.2 %all-gather.2.cloned.1.call-start = ((), (), s32[]{:S(2)}) async-start(), calls=%async_computation.1 | async-start | bytes 2048000 | tf_op jit(solution)/shard_map/all_gather | solution.py:93
  19.4 2.4 copy-start.2
  57.8 16.6 %all-to-all-start = ((bf16[8,2,25600]{2,1,0:T(2,128)(2,1)}), bf16[8,2,25600]{2,1,0:T(2,128)(2,1)S(1)}, u32[]{:S(2)}, u32[]{:S(2)}) async-start(bf16[8,2,25600]{2,1,0:T(2,128)(2,1)} %reshape.583), calls=%async_computation | async-start | bytes 1638400 | tf_op jit(solution)/shard_map/all_to_all | solution.py:13
  90.6 3.8 %copy-start.1 = (f32[1,1616,200,2]{1,2,3,0:T(8,128)S(1)}, f32[1,1616,200,2]{1,2,3,0:T(8,128)}, u32[]{:S(2)}) copy-start(f32[1,1616,200,2]{1,2,3,0:T(8,128)} %copy.18) | copy-start | bytes 7756804 | tf_op jit(solution)/shard_map/while
  112.1 3.8 %copy-start.1 = (f32[1,1616,200,2]{1,2,3,0:T(8,128)S(1)}, f32[1,1616,200,2]{1,2,3,0:T(8,128)}, u32[]{:S(2)}) copy-start(f32[1,1616,200,2]{1,2,3,0:T(8,128)} %copy.18) | copy-start | bytes 7756804 | tf_op jit(solution)/shard_map/while
  133.5 3.8 %copy-start.1 = (f32[1,1616,200,2]{1,2,3,0:T(8,128)S(1)}, f32[1,1616,200,2]{1,2,3,0:T(8,128)}, u32[]{:S(2)}) copy-start(f32[1,1616,200,2]{1,2,3,0:T(8,128)} %copy.18) | copy-start | bytes 7756804 | tf_op jit(solution)/shard_map/while
  154.9 3.8 %copy-start.1 = (f32[1,1616,200,2]{1,2,3,0:T(8,128)S(1)}, f32[1,1616,200,2]{1,2,3,0:T(8,128)}, u32[]{:S(2)}) copy-start(f32[1,1616,200,2]{1,2,3,0:T(8,128)} %copy.18) | copy-start | bytes 7756804 | tf_op jit(solution)/shard_map/while
  176.4 3.8 %copy-start.1 = (f32[1,1616,200,2]{1,2,3,0:T(8,128)S(1)}, f32[1,1616,200,2]{1,2,3,0:T(8,128)}, u32[]{:S(2)}) copy-start(f32[1,1616,200,2]{1,2,3,0:T(8,128)} %copy.18) | copy-start | bytes 7756804 | tf_op jit(solution)/shard_map/while
  197.8 3.8 %copy-start.1 = (f32[1,1616,200,2]{1,2,3,0:T(8,128)S(1)}, f32[1,1616,200,2]{1,2,3,0:T(8,128)}, u32[]{:S(2)}) copy-start(f32[1,1616,200,2]{1,2,3,0:T(8,128)} %copy.18) | copy-start | bytes 7756804 | tf_op jit(solution)/shard_map/while
  219.2 3.8 %copy-start.1 = (f32[1,1616,200,2]{1,2,3,0:T(8,128)S(1)}, f32[1,1616,200,2]{1,2,3,0:T(8,128)}, u32[]{:S(2)}) copy-start(f32[1,1616,200,2]{1,2,3,0:T(8,128)} %copy.18) | copy-start | bytes 7756804 | tf_op jit(solution)/shard_map/while
  240.7 3.8 %copy-start.1 = (f32[1,1616,200,2]{1,2,3,0:T(8,128)S(1)}, f32[1,1616,200,2]{1,2,3,0:T(8,128)}, u32[]{:S(2)}) copy-start(f32[1,1616,200,2]{1,2,3,0:T(8,128)} %copy.18) | copy-start | bytes 7756804 | tf_op jit(solution)/shard_map/while
Sparse Core Ops, SparseCore 0:
  8.9 40.8 all-gather.1
